TPU v7x, 32 devices: a whole 2x2x4 slice. The times are simulated.
32 devices in a mesh: dp: 8 (over y, x, core), mp: 4 (over z).
Axes of the slice: x: 2, y: 2, z: 4, core: 2. Of those that a mesh axis runs over, the one named last changes fastest.
Arguments:
- token_ids: int32 [16], replicated, may hold values from 0 to 3071
- cache_lengths: int32 [16], P('dp'), may hold values from 1 to 512
- embedding: bfloat16 [3072, 12288], P(('dp', 'mp')), may hold values from -6 to 6
- ln_gain: float32 [12288], replicated, may hold values from 0.25 to 1.75
- query_weight: bfloat16 [12288, 6144], P('dp', 'mp'), may hold values from -0.0546875 to 0.0546875
- key_cache: bfloat16 [16, 512, 6144], P('dp', None, 'mp'), may hold values from -1000 to 1000
- value_cache: bfloat16 [16, 512, 6144], P('dp', None, 'mp'), may hold values from -6 to 6
- out_weight: bfloat16 [6144, 12288], P('mp', 'dp'), may hold values from -0.078125 to 0.078125
- final_gain: float32 [12288], replicated, may hold values from 0.25 to 1.75
Outputs:
- log_probs: float32 [16, 3072], P(None, ('dp', 'mp'))
All inputs are finite; a program needn't handle non-finite values.
Results may differ from a plain program's by a relative error of at most 0.00033.
Values may be sent and summed in bfloat16 or wider, within the bound.
A program may use at most 128 MiB of HBM per device.

v0:
```python
import jax
import jax.numpy as jnp
from jax import lax
from jax.sharding import PartitionSpec as P

HD = 128


def per_device(
    token_ids,
    cache_lengths,
    embedding,
    ln_gain,
    query_weight,
    key_cache,
    value_cache,
    out_weight,
    final_gain,
):
    voc_rows = embedding.shape[0]
    model_width = embedding.shape[1]
    vocab_start = lax.axis_index(("dp", "mp")) * voc_rows
    one_hot = (token_ids[:, None] - vocab_start == jnp.arange(voc_rows)[None, :]).astype(
        jnp.bfloat16
    )
    partial_rows = jnp.dot(one_hot, embedding, preferred_element_type=jnp.float32)
    seq_here = key_cache.shape[0]
    cache_len = key_cache.shape[1]
    cols_here = out_weight.shape[1]
    dp_index = lax.axis_index("dp")
    block_sums = lax.psum_scatter(
        partial_rows.astype(jnp.bfloat16), "dp", scatter_dimension=1, tiled=True
    )
    embedded_cols = lax.psum(block_sums, "mp").astype(jnp.float32)
    first_sum, first_sq = lax.psum(
        (jnp.sum(embedded_cols, axis=-1), jnp.sum(embedded_cols * embedded_cols, axis=-1)), "dp"
    )
    first_mean = first_sum / model_width
    first_var = first_sq / model_width - first_mean * first_mean
    ln_here = lax.dynamic_slice_in_dim(ln_gain, dp_index * cols_here, cols_here, 0)
    normed_cols = (
        ln_here * (embedded_cols - first_mean[:, None]) * lax.rsqrt(first_var[:, None] + 1e-05)
    ).astype(jnp.bfloat16)
    own_rows = lax.all_to_all(normed_cols, "dp", split_axis=0, concat_axis=1, tiled=True)
    query_sum = jnp.dot(
        own_rows,
        lax.all_gather(query_weight, "dp", axis=0, tiled=True),
        preferred_element_type=jnp.float32,
    )
    queries = (query_sum * HD ** (-0.5)).astype(jnp.bfloat16)
    heads_here = queries.shape[1] // HD
    head_query = queries.reshape(seq_here, heads_here, HD)
    key_heads = key_cache.reshape(seq_here, cache_len, heads_here, HD)
    value_heads = value_cache.reshape(seq_here, cache_len, heads_here, HD)
    scores = jnp.einsum("shd,sthd->sht", head_query, key_heads, preferred_element_type=jnp.float32)
    live_mask = jnp.arange(cache_len)[None, None, :] < cache_lengths[:, None, None]
    scores = jnp.where(live_mask, scores, jnp.float32(-1e30))
    row_top = jnp.max(scores, axis=-1, keepdims=True)
    exp_terms = jnp.exp(scores - row_top)
    weights = (exp_terms / jnp.sum(exp_terms, axis=-1, keepdims=True)).astype(jnp.bfloat16)
    attended = jnp.einsum("sht,sthd->shd", weights, value_heads, preferred_element_type=jnp.float32)
    attended = attended.astype(jnp.bfloat16).reshape(seq_here, heads_here * HD)
    every_seq = lax.all_gather(attended, "dp", axis=0, tiled=True)
    mixed_out = lax.psum(jnp.dot(every_seq, out_weight, preferred_element_type=jnp.float32), "mp")
    hidden = embedded_cols + mixed_out
    row_sum, row_sq = lax.psum((jnp.sum(hidden, axis=-1), jnp.sum(hidden * hidden, axis=-1)), "dp")
    row_mean = row_sum / model_width
    row_var = row_sq / model_width - row_mean * row_mean
    gain_here = lax.dynamic_slice_in_dim(final_gain, dp_index * cols_here, cols_here, 0)
    final_normed = (
        gain_here * (hidden - row_mean[:, None]) * lax.rsqrt(row_var[:, None] + 1e-05)
    ).astype(jnp.bfloat16)
    logits = lax.dot_general(
        lax.all_gather(final_normed, "dp", axis=1, tiled=True),
        embedding,
        (((1,), (1,)), ((), ())),
        preferred_element_type=jnp.float32,
    )
    local_top = jnp.max(logits, axis=-1)
    global_top = lax.pmax(local_top, ("dp", "mp"))
    total_exp = lax.psum(jnp.sum(jnp.exp(logits - global_top[:, None]), axis=-1), ("dp", "mp"))
    return logits - global_top[:, None] - jnp.log(total_exp)[:, None]


def solution(mesh):
    return jax.shard_map(
        per_device,
        mesh=mesh,
        in_specs=(
            P(),
            P("dp"),
            P(("dp", "mp"), None),
            P(),
            P("dp", "mp"),
            P("dp", None, "mp"),
            P("dp", None, "mp"),
            P("mp", "dp"),
            P(),
        ),
        out_specs=P(None, ("dp", "mp")),
        check_vma=False,
    )
```

profile of v0, /device:TPU:0, one launch (start us, length us, event | category | flops | bytes accessed | tf_op | source)
XLA Modules:
  0.0 406.1 jit_solution(14732259672830846114)
XLA Ops:
  6.5 0.8 broadcast_subtract_fusion
  7.3 0.9 copy-done
  8.2 1.2 convolution_convert_fusion
  11.0 36.0 %reduce-scatter.2.cloned.1.call-done = bf16[16,1536]{1,0:T(8,128)(2,1)} async-done(((bf16[16,12288]{1,0:T(8,128)(2,1)}), bf16[16,1536]{1,0:T(8,128)(2,1)}) %reduce-scatter.2.cloned.1.call-update) | async-done | bytes 49168 | tf_op jit(solution)/shard_map/reduce_scatter | solution.py:31
  47.0 19.9 %psum.49 = bf16[16,1536]{1,0:T(8,128)(2,1)S(1)} all-reduce(bf16[16,1536]{1,0:T(8,128)(2,1)} %reduce-scatter.2.cloned.1.call-done), channel_id=1, replica_groups=mesh['dp'=8,'mp'=4] {'mp'}, use_global_device_ids=true, to_apply=%region_1.0 | all-reduce | flops 24576 | bytes 98304 | tf_op jit(solution)/shard_map/psum | solution.py:34
  67.1 12.8 %all-reduce.1 = (f32[16]{0:T(128)S(1)}, f32[16]{0:T(128)S(1)}) all-reduce(f32[16]{0:T(128)S(1)} %get-tuple-element.8, f32[16]{0:T(128)S(1)} %get-tuple-element.7), channel_id=1, replica_groups=mesh['dp'=8,'mp'=4] {'dp'}, use_global_device_ids=true, to_apply=%region_5.0 | all-reduce | flops 32 | bytes 256 | tf_op jit(solution)/shard_map/psum | solution.py:35
  80.6 3.3 all-to-all-start
  84.1 4.7 %copy.14 = bf16[2,512,1536]{1,2,0:T(8,128)(2,1)} copy(bf16[2,512,1536]{2,1,0:T(8,128)(2,1)} %param.14) | data formatting | bytes 6291456 | tf_op args[5]
  88.8 4.7 %copy.15 = bf16[2,512,1536]{1,2,0:T(8,128)(2,1)} copy(bf16[2,512,1536]{2,1,0:T(8,128)(2,1)} %param.15) | data formatting | bytes 6291456 | tf_op args[6]
  93.4 135.6 %all-gather.3.cloned.1.call-done = bf16[12288,1536]{1,0:T(8,128)(2,1)} async-done(((bf16[1536,1536]{1,0:T(8,128)(2,1)}), bf16[12288,1536]{1,0:T(8,128)(2,1)}) %all-gather.3.cloned.1.call-update) | async-done | bytes 37748752 | tf_op jit(solution)/shard_map/all_gather | solution.py:47
  229.1 14.3 %fusion.2 = bf16[2,1536]{1,0:T(2,128)(2,1)S(1)} fusion(bf16[2,12288]{1,0:T(2,128)(2,1)S(1)} %bitcast.29, bf16[12288,1536]{1,0:T(8,128)(2,1)} %all-gather.3.cloned.1.call-done), kind=kOutput, calls=%fused_computation.4 | convolution fusion | flops 75503616 | bytes 37804032 | tf_op jit(solution)/shard_map/dot_general | solution.py:45
  243.4 2.4 fusion.20
  246.0 2.8 fusion.12
  248.8 9.1 %all-gather = bf16[8,2,1536]{2,1,0:T(2,128)(2,1)S(1)} all-gather(bf16[1,2,1536]{2,1,0:T(2,128)(2,1)S(1)} %reshape.56), channel_id=1, replica_groups=mesh['dp'=8,'mp'=4] {'dp'}, dimensions={0}, use_global_device_ids=true | all-gather | bytes 55296 | tf_op jit(solution)/shard_map/all_gather | solution.py:63
  258.0 3.7 fusion.21
  261.7 0.8 dynamic_slice.6
  262.5 33.8 %all-reduce.4.cloned.1.call-done = f32[16,1536]{1,0:T(8,128)} async-done(((f32[16,1536]{1,0:T(8,128)}), f32[16,1536]{1,0:T(8,128)}) %all-reduce.4.cloned.1.call-update) | async-done | bytes 98320 | tf_op jit(solution)/shard_map/psum | solution.py:64
  296.3 1.0 fusion.14
  297.3 11.8 %all-reduce = (f32[16]{0:T(128)S(1)}, f32[16]{0:T(128)S(1)}) all-reduce(f32[16]{0:T(128)S(1)} %get-tuple-element.6, f32[16]{0:T(128)S(1)} %get-tuple-element.5), channel_id=1, replica_groups=mesh['dp'=8,'mp'=4] {'dp'}, use_global_device_ids=true, to_apply=%region_12.13 | all-reduce | flops 32 | bytes 256 | tf_op jit(solution)/shard_map/psum | solution.py:66
  309.2 1.0 multiply_convert_fusion
  310.1 9.5 %all_gather.11 = bf16[16,12288]{1,0:T(8,128)(2,1)S(1)} all-gather(bf16[16,1536]{1,0:T(8,128)(2,1)S(1)} %multiply_convert_fusion), channel_id=1, replica_groups=mesh['dp'=8,'mp'=4] {'dp'}, dimensions={1}, use_global_device_ids=true | all-gather | bytes 442368 | tf_op jit(solution)/shard_map/all_gather | solution.py:74
  319.7 0.8 fusion.19
  320.5 39.2 %pmax.7 = f32[16]{0:T(128)S(1)} all-reduce(f32[16]{0:T(128)S(1)} %get-tuple-element.17), channel_id=1, replica_groups=mesh['dp'=8,'mp'=4] {'dp','mp'}, use_global_device_ids=true, to_apply=%region_14.15 | all-reduce | flops 16 | bytes 128 | tf_op jit(solution)/shard_map/pmax | solution.py:80
  359.9 39.0 %psum.55 = f32[16]{0:T(128)S(1)} all-reduce(f32[16]{0:T(128)S(1)} %exponential_reduce_fusion), channel_id=1, replica_groups=mesh['dp'=8,'mp'=4] {'dp','mp'}, use_global_device_ids=true, to_apply=%region_16.17 | all-reduce | flops 16 | bytes 128 | tf_op jit(solution)/shard_map/psum | solution.py:81
  (25 shorter events, 3.7 us)
Async XLA Ops:
  6.5 1.7 copy-start
  6.5 40.5 %reduce-scatter.2.cloned.1.call-start = ((), (), s32[]{:S(2)}) async-start(), calls=%async_computation.2 | async-start | bytes 442368 | tf_op jit(solution)/shard_map/reduce_scatter | solution.py:31
  9.5 74.5 %copy-start.1 = (s32[2]{0:T(128)S(1)}, s32[2]{0:T(128)}, u32[]{:S(2)}) copy-start(s32[2]{0:T(128)} %param.10) | copy-start | bytes 28
  9.5 219.6 %all-gather.3.cloned.1.call-start = ((), (), s32[]{:S(2)}) async-start(), calls=%async_computation.3 | async-start | bytes 42467328 | tf_op jit(solution)/shard_map/all_gather | solution.py:47
  80.6 12.9 %all-to-all-start = ((bf16[8,2,1536]{2,1,0:T(2,128)(2,1)}), bf16[8,2,1536]{2,1,0:T(2,128)(2,1)S(1)}, u32[]{:S(2)}, u32[]{:S(2)}) async-start(bf16[8,2,1536]{2,1,0:T(2,128)(2,1)} %all_to_all.14), calls=%async_computation.1 | async-start | bytes 98304 | tf_op jit(solution)/shard_map/all_to_all | solution.py:44
  83.9 212.4 %all-reduce.4.cloned.1.call-start = ((), (), s32[]{:S(2)}) async-start(), calls=%async_computation.4 | async-start | bytes 196608 | tf_op jit(solution)/shard_map/psum | solution.py:64
Sparse Core Ops, SparseCore 0:
  10.4 36.5 reduce-scatter.1
  48.9 180.1 all-gather.2
  261.8 34.4 all-reduce.3
where the time goes:
time: 407 us; the launch traced here: 406 us
  waiting for transfers between devices  206 us (51%)
  blocking collectives  141 us (35%)
  matrix products  25.2 us (6%)
  between operations  13.2 us (3%)
  local copies, waits for them, and re-layouts  12.6 us (3%)
  other arithmetic  4.18 us (1%)
    all_gather x1, waiting for transfers between devices, per_device(): lax.all_gather(query_weight, 'dp', axis=0, tiled=True)  136 us
    pmax x1, blocking collectives, per_device(): global_top = lax.pmax(local_top, ('dp', 'mp'))  39.2 us
    psum x1, blocking collectives, per_device(): lax.psum(jnp.sum(jnp.exp(logits - global_top[:, None]), axis=-1), ('dp',...  39 us
    reduce_scatter x1, waiting for transfers between devices, per_device(): lax.psum_scatter(partial_rows.astype(jnp.bfloat16), 'dp', scatter_dimensi...  36 us
    psum x1, waiting for transfers between devices, per_device(): lax.psum(jnp.dot(every_seq, out_weight, preferred_element_type=jnp.float3...  33.8 us
    psum x1, blocking collectives, per_device(): embedded_cols = lax.psum(block_sums, 'mp').astype(jnp.float32)  19.9 us
    dot_general x1, matrix products, per_device(): jnp.dot(own_rows, lax.all_gather(query_weight, 'dp', axis=0, tiled=True),...  14.3 us
    psum x1, blocking collectives, per_device(): lax.psum((jnp.sum(embedded_cols, axis=-1), jnp.sum(embedded_cols * embedd...  12.8 us
  transfers between devices with their start and end apart: 4, of which 3 were waited for; matrix products, arithmetic and copies ran while one was open for 3% of the time, Pallas kernels for 0%

commit v1 on v0

--- a/solution.py
+++ b/solution.py
@@ -78,7 +78,9 @@
     )
     local_top = jnp.max(logits, axis=-1)
     global_top = lax.pmax(local_top, ("dp", "mp"))
-    total_exp = lax.psum(jnp.sum(jnp.exp(logits - global_top[:, None]), axis=-1), ("dp", "mp"))
+    total_exp = lax.psum(
+        lax.psum(jnp.sum(jnp.exp(logits - global_top[:, None]), axis=-1), "dp"), "mp"
+    )
     return logits - global_top[:, None] - jnp.log(total_exp)[:, None]
 
 

time: 407 us -> 391 us (0.961)
  blocking collectives: 141 us -> 126 us
    psum x1 -> x2, blocking collectives: 39 us -> 23.1 us  [the longest x1 12.7 us: per_device(): lax.psum(jnp.sum(jnp.exp(logits - global_top[:, None]), axis=-1), 'dp')]
where the time goes in v1:
time: 391 us; the launch traced here: 390 us
  waiting for transfers between devices  206 us (53%)
  blocking collectives  126 us (32%)
  matrix products  25.2 us (6%)
  between operations  13.2 us (3%)
  local copies, waits for them, and re-layouts  12.6 us (3%)
  other arithmetic  4.18 us (1%)
    all_gather x1, waiting for transfers between devices, per_device(): lax.all_gather(query_weight, 'dp', axis=0, tiled=True)  136 us
    pmax x1, blocking collectives, per_device(): global_top = lax.pmax(local_top, ('dp', 'mp'))  39.2 us
    reduce_scatter x1, waiting for transfers between devices, per_device(): lax.psum_scatter(partial_rows.astype(jnp.bfloat16), 'dp', scatter_dimensi...  36 us
    psum x1, waiting for transfers between devices, per_device(): lax.psum(jnp.dot(every_seq, out_weight, preferred_element_type=jnp.float3...  33.8 us
    psum x1, blocking collectives, per_device(): embedded_cols = lax.psum(block_sums, 'mp').astype(jnp.float32)  19.9 us
    dot_general x1, matrix products, per_device(): jnp.dot(own_rows, lax.all_gather(query_weight, 'dp', axis=0, tiled=True),...  14.3 us
    psum x1, blocking collectives, per_device(): lax.psum((jnp.sum(embedded_cols, axis=-1), jnp.sum(embedded_cols * embedd...  12.8 us
    psum x1, blocking collectives, per_device(): lax.psum(jnp.sum(jnp.exp(logits - global_top[:, None]), axis=-1), 'dp')  12.7 us
  transfers between devices with their start and end apart: 4, of which 3 were waited for; matrix products, arithmetic and copies ran while one was open for 3% of the time, Pallas kernels for 0%

profile of v1, /device:TPU:0, one launch (start us, length us, event | category | flops | bytes accessed | tf_op | source)
XLA Modules:
  0.0 390.3 jit_solution(4034430911282069510)
XLA Ops:
  6.5 0.8 broadcast_subtract_fusion
  7.3 0.9 copy-done
  8.2 1.2 convolution_convert_fusion
  11.0 36.0 %reduce-scatter.2.cloned.1.call-done = bf16[16,1536]{1,0:T(8,128)(2,1)} async-done(((bf16[16,12288]{1,0:T(8,128)(2,1)}), bf16[16,1536]{1,0:T(8,128)(2,1)}) %reduce-scatter.2.cloned.1.call-update) | async-done | bytes 49168 | tf_op jit(solution)/shard_map/reduce_scatter | solution.py:31
  47.0 19.9 %psum.56 = bf16[16,1536]{1,0:T(8,128)(2,1)S(1)} all-reduce(bf16[16,1536]{1,0:T(8,128)(2,1)} %reduce-scatter.2.cloned.1.call-done), channel_id=1, replica_groups=mesh['dp'=8,'mp'=4] {'mp'}, use_global_device_ids=true, to_apply=%region_1.0 | all-reduce | flops 24576 | bytes 98304 | tf_op jit(solution)/shard_map/psum | solution.py:34
  67.1 12.8 %all-reduce.1 = (f32[16]{0:T(128)S(1)}, f32[16]{0:T(128)S(1)}) all-reduce(f32[16]{0:T(128)S(1)} %get-tuple-element.8, f32[16]{0:T(128)S(1)} %get-tuple-element.7), channel_id=1, replica_groups=mesh['dp'=8,'mp'=4] {'dp'}, use_global_device_ids=true, to_apply=%region_5.0 | all-reduce | flops 32 | bytes 256 | tf_op jit(solution)/shard_map/psum | solution.py:35
  80.6 3.3 all-to-all-start
  84.1 4.7 %copy.14 = bf16[2,512,1536]{1,2,0:T(8,128)(2,1)} copy(bf16[2,512,1536]{2,1,0:T(8,128)(2,1)} %param.14) | data formatting | bytes 6291456 | tf_op args[5]
  88.8 4.7 %copy.15 = bf16[2,512,1536]{1,2,0:T(8,128)(2,1)} copy(bf16[2,512,1536]{2,1,0:T(8,128)(2,1)} %param.15) | data formatting | bytes 6291456 | tf_op args[6]
  93.4 135.6 %all-gather.3.cloned.1.call-done = bf16[12288,1536]{1,0:T(8,128)(2,1)} async-done(((bf16[1536,1536]{1,0:T(8,128)(2,1)}), bf16[12288,1536]{1,0:T(8,128)(2,1)}) %all-gather.3.cloned.1.call-update) | async-done | bytes 37748752 | tf_op jit(solution)/shard_map/all_gather | solution.py:47
  229.1 14.3 %fusion.2 = bf16[2,1536]{1,0:T(2,128)(2,1)S(1)} fusion(bf16[2,12288]{1,0:T(2,128)(2,1)S(1)} %bitcast.29, bf16[12288,1536]{1,0:T(8,128)(2,1)} %all-gather.3.cloned.1.call-done), kind=kOutput, calls=%fused_computation.4 | convolution fusion | flops 75503616 | bytes 37804032 | tf_op jit(solution)/shard_map/dot_general | solution.py:45
  243.4 2.4 fusion.20
  246.0 2.8 fusion.12
  248.8 9.1 %all-gather = bf16[8,2,1536]{2,1,0:T(2,128)(2,1)S(1)} all-gather(bf16[1,2,1536]{2,1,0:T(2,128)(2,1)S(1)} %reshape.56), channel_id=1, replica_groups=mesh['dp'=8,'mp'=4] {'dp'}, dimensions={0}, use_global_device_ids=true | all-gather | bytes 55296 | tf_op jit(solution)/shard_map/all_gather | solution.py:63
  258.0 3.7 fusion.21
  262.5 33.8 %all-reduce.4.cloned.1.call-done = f32[16,1536]{1,0:T(8,128)} async-done(((f32[16,1536]{1,0:T(8,128)}), f32[16,1536]{1,0:T(8,128)}) %all-reduce.4.cloned.1.call-update) | async-done | bytes 98320 | tf_op jit(solution)/shard_map/psum | solution.py:64
  296.3 1.0 fusion.14
  297.3 11.8 %all-reduce = (f32[16]{0:T(128)S(1)}, f32[16]{0:T(128)S(1)}) all-reduce(f32[16]{0:T(128)S(1)} %get-tuple-element.6, f32[16]{0:T(128)S(1)} %get-tuple-element.5), channel_id=1, replica_groups=mesh['dp'=8,'mp'=4] {'dp'}, use_global_device_ids=true, to_apply=%region_12.13 | all-reduce | flops 32 | bytes 256 | tf_op jit(solution)/shard_map/psum | solution.py:66
  309.2 1.0 multiply_convert_fusion
  310.1 9.5 %all_gather.11 = bf16[16,12288]{1,0:T(8,128)(2,1)S(1)} all-gather(bf16[16,1536]{1,0:T(8,128)(2,1)S(1)} %multiply_convert_fusion), channel_id=1, replica_groups=mesh['dp'=8,'mp'=4] {'dp'}, dimensions={1}, use_global_device_ids=true | all-gather | bytes 442368 | tf_op jit(solution)/shard_map/all_gather | solution.py:74
  319.7 0.8 fusion.19
  320.5 39.2 %pmax.7 = f32[16]{0:T(128)S(1)} all-reduce(f32[16]{0:T(128)S(1)} %get-tuple-element.17), channel_id=1, replica_groups=mesh['dp'=8,'mp'=4] {'dp','mp'}, use_global_device_ids=true, to_apply=%region_14.15 | all-reduce | flops 16 | bytes 128 | tf_op jit(solution)/shard_map/pmax | solution.py:80
  359.9 12.7 %psum.62 = f32[16]{0:T(128)S(1)} all-reduce(f32[16]{0:T(128)S(1)} %exponential_reduce_fusion), channel_id=1, replica_groups=mesh['dp'=8,'mp'=4] {'dp'}, use_global_device_ids=true, to_apply=%region_16.17 | all-reduce | flops 16 | bytes 128 | tf_op jit(solution)/shard_map/psum | solution.py:82
  372.6 10.4 %psum.63 = f32[16]{0:T(128)S(1)} all-reduce(f32[16]{0:T(128)S(1)} %psum.62), channel_id=1, replica_groups=mesh['dp'=8,'mp'=4] {'mp'}, use_global_device_ids=true, to_apply=%region_17.18 | all-reduce | flops 16 | bytes 128 | tf_op jit(solution)/shard_map/psum | solution.py:81
  (26 shorter events, 4.5 us)
Async XLA Ops:
  6.5 1.7 copy-start
  6.5 40.5 %reduce-scatter.2.cloned.1.call-start = ((), (), s32[]{:S(2)}) async-start(), calls=%async_computation.2 | async-start | bytes 442368 | tf_op jit(solution)/shard_map/reduce_scatter | solution.py:31
  9.5 74.5 %copy-start.1 = (s32[2]{0:T(128)S(1)}, s32[2]{0:T(128)}, u32[]{:S(2)}) copy-start(s32[2]{0:T(128)} %param.10) | copy-start | bytes 28
  9.5 219.6 %all-gather.3.cloned.1.call-start = ((), (), s32[]{:S(2)}) async-start(), calls=%async_computation.3 | async-start | bytes 42467328 | tf_op jit(solution)/shard_map/all_gather | solution.py:47
  80.6 12.9 %all-to-all-start = ((bf16[8,2,1536]{2,1,0:T(2,128)(2,1)}), bf16[8,2,1536]{2,1,0:T(2,128)(2,1)S(1)}, u32[]{:S(2)}, u32[]{:S(2)}) async-start(bf16[8,2,1536]{2,1,0:T(2,128)(2,1)} %all_to_all.14), calls=%async_computation.1 | async-start | bytes 98304 | tf_op jit(solution)/shard_map/all_to_all | solution.py:44
  83.9 212.4 %all-reduce.4.cloned.1.call-start = ((), (), s32[]{:S(2)}) async-start(), calls=%async_computation.4 | async-start | bytes 196608 | tf_op jit(solution)/shard_map/psum | solution.py:64
Sparse Core Ops, SparseCore 0:
  10.4 36.5 reduce-scatter.1
  48.9 180.1 all-gather.2
  261.8 34.4 all-reduce.3
